TPU v7x, 256 devices: a whole 4x4x8 slice. The times are simulated.
256 devices in a mesh: freq: 4 (over x_hi, core), rcv: 64 (over y, z, x_lo).
Axes of the slice: x: 4 (x_hi: 2, x_lo: 2; x = x_hi * 2 + x_lo), y: 4, z: 8, core: 2. Of those that a mesh axis runs over, the one named last changes fastest.
Arguments:
- reflection: bfloat16 [8, 2, 2560, 2560], P('freq', None, 'rcv'), may hold values from -5 to 5, as said below
- starts: int32 [2560, 192], P('rcv'), may hold values from 8 to 56
- focusing: float32 [8, 2560, 2, 192], P('freq', 'rcv'), may hold values from -6 to 6
- residual: float32 [8, 2560, 2, 192], P('freq', 'rcv'), may hold values from -6 to 6
- direction: float32 [8, 2560, 2, 192], P('freq', 'rcv'), may hold values from -6 to 6
- gradient: float32 [8, 2560, 2, 192], P('freq', 'rcv'), may hold values from -30 to 30
Outputs:
- new_focusing: float32 [8, 2560, 2, 192], P('freq', 'rcv')
- new_residual: float32 [8, 2560, 2, 192], P('freq', 'rcv')
- new_direction: float32 [8, 2560, 2, 192], P('freq', 'rcv')
- green_field: float32 [8, 2560, 2, 192], P('freq', 'rcv')
- focal_correlation: float32 [8, 2, 192], P('freq')
Inputs may be any that keep to these rules, and one draw needn't show every extreme that they name: Each frequency's matrix is symmetric in source and receiver: reflection[f, c, s, r] = reflection[f, c, r, s].
All inputs are finite; a program needn't handle non-finite values.
Results may differ from a plain program's by a relative error of at most 0.0003.
The roundings to bfloat16 on the way count: a program that leaves them out, or rounds other values in their place, can miss the bound.
Values may be sent and summed in bfloat16 or wider, within the bound.
A program may use at most 64 MiB of HBM per device.

v0:
```python
import math
import jax
import jax.numpy as jnp
from jax import lax
from jax.sharding import Mesh
from jax.sharding import PartitionSpec as P

N = 2560
F = 8
TS = 64
FREQ = ("freq_0", "freq_1")
RCV = ("rcv_0", "rcv_1", "rcv_2")
FREQ_RCV = ("freq_0", "freq_1", "rcv_0", "rcv_1", "rcv_2")
band_start = 5
tiny = 1e-06
highest = lax.Precision.HIGHEST


def in_order(pieces, dim):
    lengths = list(pieces.shape[1:])
    lengths[dim] *= pieces.shape[0]
    return jnp.moveaxis(pieces, 0, dim).reshape(lengths)


def sent_to_all(value, axis):
    count = lax.axis_size(axis)
    return lax.all_to_all(
        jnp.broadcast_to(value[None], (count, *value.shape)), axis, 0, 0, tiled=True
    )


def gather_directly(value, axis, dim):
    return in_order(sent_to_all(value, axis), dim)


def one_axis_at_a_time(value, axes):
    for axis in axes:
        value = lax.psum(value, axis)
    return value


def all_blocks(value, axes, sequence):
    pieces = value
    for k in sequence:
        pieces = lax.all_gather(pieces, axes[k])
    done = sequence[::-1]
    back = [done.index(k) for k in range(len(axes))]
    pieces = pieces.transpose(*back, *range(len(axes), pieces.ndim))
    return pieces.reshape(-1, *value.shape)


def gathered_by_axis(value, axes, sequence, dim):
    return in_order(all_blocks(value, axes, sequence), dim)


def of_everyone(value, axis):
    everything = sent_to_all(value, axis)
    return jnp.sum(everything, axis=0)


def tables(count, offset):
    times = jnp.arange(TS, dtype=jnp.float32)[:, None]
    bins = (jnp.arange(count, dtype=jnp.int32) + offset + band_start).astype(jnp.float32)[None, :]
    phase = 2.0 * jnp.pi * times * bins / TS
    return (jnp.cos(phase), jnp.sin(phase))


def contract_time(table, values):
    return jnp.einsum("tf,frk->trk", table, values, precision=highest)


def contract_back(table, values):
    return jnp.einsum("tf,trk->frk", table, values, precision=highest)


def time_gate(field, forward_cos, forward_sin, back_cos, back_sin, limits, complement):
    real_part = field[:, :, 0]
    imag_part = field[:, :, 1]
    time_real = contract_time(forward_cos, real_part) - contract_time(forward_sin, imag_part)
    time_imag = contract_time(forward_sin, real_part) + contract_time(forward_cos, imag_part)
    clock = jnp.arange(TS, dtype=jnp.int32)[:, None, None]
    window = (clock < limits[None]).astype(jnp.float32)
    if complement:
        window = 1.0 - window
    kept_real = window * time_real
    kept_imag = window * time_imag
    out_real = (contract_back(back_cos, kept_real) + contract_back(back_sin, kept_imag)) / TS
    out_imag = (contract_back(back_cos, kept_imag) - contract_back(back_sin, kept_real)) / TS
    return jnp.stack([out_real, out_imag], axis=2)


def combine(total, conjugate):
    if conjugate:
        out_real = total[:, 0, :, 0] + total[:, 1, :, 1]
        out_imag = total[:, 0, :, 1] - total[:, 1, :, 0]
    else:
        out_real = total[:, 0, :, 0] - total[:, 1, :, 1]
        out_imag = total[:, 0, :, 1] + total[:, 1, :, 0]
    return jnp.stack([out_real, out_imag], axis=2)


def per_device(reflection, starts, focusing, residual, direction, gradient):
    local_freq = reflection.shape[0]
    position = lax.axis_index(FREQ)
    cos_table, sin_table = tables(F, 0)
    own_cos, own_sin = tables(local_freq, position * local_freq)

    def gate(field, complement):
        whole = gather_directly(field, FREQ, 0)
        return time_gate(whole, cos_table, sin_table, own_cos, own_sin, starts, complement)

    def accumulate(piece):
        return jnp.einsum("fpnm,fmqk->fpnqk", reflection, piece, preferred_element_type=jnp.float32)

    direction_low = direction.astype(jnp.bfloat16)
    focusing_low = focusing.astype(jnp.bfloat16)
    aimed_total = accumulate(lax.all_gather(direction_low, RCV, axis=1, tiled=True))
    direction_image = combine(aimed_total, False)
    image = gate(direction_image, False)
    gamma, curvature = (
        one_axis_at_a_time(jnp.sum(gradient * gradient), FREQ_RCV),
        one_axis_at_a_time(jnp.sum(image * image), FREQ_RCV),
    )
    alpha = gamma / (curvature + tiny)
    new_focusing = focusing + alpha * direction
    new_residual = residual - alpha * image
    gated = gate(new_residual, False).astype(jnp.bfloat16)
    total = accumulate(gathered_by_axis(gated, RCV, (2, 0, 1), 1))
    new_gradient = combine(total, True)
    new_gamma = one_axis_at_a_time(jnp.sum(new_gradient * new_gradient), FREQ_RCV)
    new_direction = new_gradient + new_gamma / (gamma + tiny) * direction
    focus_total = accumulate(lax.all_gather(focusing_low, RCV, axis=1, tiled=True))
    focusing_image = combine(focus_total, False)
    green_field = gate(focusing_image + alpha * direction_image, True)
    corr_real = jnp.sum(
        green_field[:, :, 0] * new_focusing[:, :, 0] + green_field[:, :, 1] * new_focusing[:, :, 1],
        axis=1,
    )
    corr_imag = jnp.sum(
        green_field[:, :, 1] * new_focusing[:, :, 0] - green_field[:, :, 0] * new_focusing[:, :, 1],
        axis=1,
    )
    partial_corr = jnp.stack([corr_real, corr_imag], axis=1)
    focal_correlation = of_everyone(partial_corr, RCV) / math.sqrt(N)
    return (new_focusing, new_residual, new_direction, green_field, focal_correlation)


def solution(mesh):
    finer = Mesh(
        mesh.devices.reshape(2, 2, 4, 8, 2), ("freq_0", "freq_1", "rcv_0", "rcv_1", "rcv_2")
    )
    in_specs = (
        P(FREQ, None, RCV, None),
        P(RCV, None),
        P(FREQ, RCV, None, None),
        P(FREQ, RCV, None, None),
        P(FREQ, RCV, None, None),
        P(FREQ, RCV, None, None),
    )
    out_specs = (
        P(FREQ, RCV, None, None),
        P(FREQ, RCV, None, None),
        P(FREQ, RCV, None, None),
        P(FREQ, RCV, None, None),
        P(FREQ, None, None),
    )
    return jax.shard_map(
        per_device, mesh=finer, in_specs=in_specs, out_specs=out_specs, check_vma=False
    )
```

profile of v0, /device:TPU:4, one launch (start us, length us, event | category | flops | bytes accessed | tf_op | source)
XLA Modules:
  0.0 782.8 jit_solution(11673476122548457123)
XLA Ops:
  7.2 1.6 copy.290
  8.9 1.6 copy.289
  10.5 307.9 %all-gather.6.cloned.1.call-done = bf16[2,2560,2,192]{3,1,2,0:T(8,128)(2,1)} async-done(((bf16[2,40,2,192]{3,1,2,0:T(8,128)(2,1)}), bf16[2,2560,2,192]{3,1,2,0:T(8,128)(2,1)}) %all-gather.6.cloned.1.call-update) | async-done | bytes 3932176 | tf_op jit(solution)/shard_map/all_gather | solution.py:117
  318.5 3.5 fusion
  323.2 4.8 all-to-all-start
  328.8 12.3 %all-to-all-done = f32[4,2,40,2,192]{4,1,2,3,0:T(2,128)S(1)} async-done(((f32[4,2,40,2,192]{4,1,2,3,0:T(2,128)}), f32[4,2,40,2,192]{4,1,2,3,0:T(2,128)S(1)}, u32[]{:S(2)}, u32[]{:S(2)}) %all-to-all-start) | async-done | bytes 491552 | tf_op jit(solution)/shard_map/all_to_all | solution.py:27
  341.8 2.4 fusion.7
  344.1 2.5 add_select_fusion.1
  346.7 1.4 fusion.115
  349.5 2.4 fusion.8
  351.8 2.5 subtract_select_fusion.1
  354.4 1.6 fusion.103
  358.0 7.1 all-reduce.4
  365.1 3.1 all-reduce.3
  368.1 8.3 %all-reduce.1 = (f32[]{:T(128)}, f32[]{:T(128)}) all-reduce(f32[]{:T(128)} %get-tuple-element.38, f32[]{:T(128)} %get-tuple-element.39), channel_id=1, replica_groups=mesh['freq_0'=2,'freq_1'=2,'rcv_0'=4,'rcv_1'=8,'rcv_2'=2] {'rcv_0'}, use_global_device_ids=true, to_apply=%region_3.0 | all-reduce | flops 2 | bytes 16 | tf_op jit(solution)/shard_map/psum | solution.py:38
  376.5 20.8 %all-reduce = (f32[]{:T(128)}, f32[]{:T(128)}) all-reduce(f32[]{:T(128)} %get-tuple-element.34, f32[]{:T(128)} %get-tuple-element.35), channel_id=1, replica_groups=mesh['freq_0'=2,'freq_1'=2,'rcv_0'=4,'rcv_1'=8,'rcv_2'=2] {'rcv_1'}, use_global_device_ids=true, to_apply=%region_4.0 | all-reduce | flops 2 | bytes 16 | tf_op jit(solution)/shard_map/psum | solution.py:38
  397.3 5.8 all-reduce.2
  405.4 18.5 %all_to_all.20 = f32[4,2,40,2,192]{4,1,2,3,0:T(2,128)S(1)} all-to-all(f32[4,2,40,2,192]{4,1,2,3,0:T(2,128)S(1)} %broadcast_in_dim.9), channel_id=1, replica_groups=mesh['freq_0'=2,'freq_1'=2,'rcv_0'=4,'rcv_1'=8,'rcv_2'=2] {'freq_0','fre..., dimensions={0} | all-to-all | bytes 983040 | tf_op jit(solution)/shard_map/all_to_all | solution.py:27
  424.6 2.4 fusion.10
  427.0 2.5 subtract_select_fusion
  429.5 1.4 fusion.99
  430.9 2.4 fusion.9
  433.3 2.5 add_select_fusion
  437.2 1.8 fusion.101
  440.4 6.1 all_gather.23
  446.6 15.6 %all-gather = bf16[8,2,40,2,192]{4,2,3,1,0:T(8,128)(2,1)} all-gather(bf16[2,2,40,2,192]{4,2,3,1,0:T(8,128)(2,1)S(1)} %all_gather.23), channel_id=2, replica_groups=mesh['freq_0'=2,'freq_1'=2,'rcv_0'=4,'rcv_1'=8,'rcv_2'=2] {'rcv_0'}, dimensions={0}, use_global_device_ids=true | all-gather | bytes 614400 | tf_op jit(solution)/shard_map/all_gather | solution.py:45
  462.2 162.9 %all-gather.8.cloned.1.call-done = bf16[2,2560,2,192]{3,1,2,0:T(8,128)(2,1)} async-done(((bf16[2,40,2,192]{3,1,2,0:T(8,128)(2,1)}), bf16[2,2560,2,192]{3,1,2,0:T(8,128)(2,1)}) %all-gather.8.cloned.1.call-update) | async-done | bytes 3932176 | tf_op jit(solution)/shard_map/all_gather | solution.py:132
  625.1 3.5 fusion.2
  629.8 4.8 all-to-all-start.2
  635.3 7.9 %all-to-all-done.2 = f32[4,2,40,2,192]{4,1,2,3,0:T(2,128)S(1)} async-done(((f32[4,2,40,2,192]{4,1,2,3,0:T(2,128)}), f32[4,2,40,2,192]{4,1,2,3,0:T(2,128)S(1)}, u32[]{:S(2)}, u32[]{:S(2)}) %all-to-all-start.2) | async-done | bytes 491552 | tf_op jit(solution)/shard_map/all_to_all | solution.py:27
  643.9 2.4 fusion.11
  646.3 3.9 fusion.12
  650.1 3.7 add_multiply_fusion
  653.8 34.5 %all-gather.10.cloned.1.call-done = bf16[32,2,2,40,2,192]{5,3,4,2,1,0:T(8,128)(2,1)} async-done(((bf16[4,2,2,40,2,192]{5,3,4,2,1,0:T(8,128)(2,1)}), bf16[32,2,2,40,2,192]{5,3,4,2,1,0:T(8,128)(2,1)}) %all-gather.10.cloned.1.call-update) | async-done | bytes 3932176 | tf_op jit(solution)/shard_map/all_gather | solution.py:45
  688.3 3.0 copy.180
  694.3 4.3 subtract_multiply_fusion
  698.6 7.1 psum.115
  705.7 3.8 fusion.109
  709.4 3.3 psum.116
  712.7 3.7 fusion.95
  716.4 11.1 %psum.117 = f32[]{:T(128)} all-reduce(f32[]{:T(128)} %psum.116), channel_id=1, replica_groups=mesh['freq_0'=2,'freq_1'=2,'rcv_0'=4,'rcv_1'=8,'rcv_2'=2] {'rcv_0'}, use_global_device_ids=true, to_apply=%region_15.0 | all-reduce | flops 1 | bytes 8 | tf_op jit(solution)/shard_map/psum | solution.py:38
  727.5 2.0 fusion.97
  729.5 16.1 %psum.118 = f32[]{:T(128)} all-reduce(f32[]{:T(128)} %psum.117), channel_id=1, replica_groups=mesh['freq_0'=2,'freq_1'=2,'rcv_0'=4,'rcv_1'=8,'rcv_2'=2] {'rcv_1'}, use_global_device_ids=true, to_apply=%region_16.0 | all-reduce | flops 1 | bytes 8 | tf_op jit(solution)/shard_map/psum | solution.py:38
  745.7 2.0 fusion.107
  747.7 5.5 psum.119
  756.9 7.5 all-to-all-start.3
  764.3 1.7 copy.198
  768.4 6.9 all-to-all-done.3
  (74 shorter events, 21.5 us)
Async XLA Ops:
  7.2 311.3 %copy-start = (bf16[2,2,40,2560]{3,2,1,0:T(8,128)(2,1)S(1)}, bf16[2,2,40,2560]{3,2,1,0:T(8,128)(2,1)}, u32[]{:S(2)}) copy-start(bf16[2,2,40,2560]{3,2,1,0:T(8,128)(2,1)} %param.6) | copy-start | bytes 2457604
  7.2 311.3 %all-gather.6.cloned.1.call-start = ((), (), s32[]{:S(2)}) async-start(), calls=%async_computation.4 | async-start | bytes 5324800 | tf_op jit(solution)/shard_map/all_gather | solution.py:117
  8.9 616.2 %all-gather.8.cloned.1.call-start = ((), (), s32[]{:S(2)}) async-start(), calls=%async_computation.5 | async-start | bytes 5324800 | tf_op jit(solution)/shard_map/all_gather | solution.py:132
  322.0 6.0 copy-start.8
  323.2 17.9 %all-to-all-start = ((f32[4,2,40,2,192]{4,1,2,3,0:T(2,128)}), f32[4,2,40,2,192]{4,1,2,3,0:T(2,128)S(1)}, u32[]{:S(2)}, u32[]{:S(2)}) async-start(f32[4,2,40,2,192]{4,1,2,3,0:T(2,128)} %broadcast_in_dim.8), calls=%async_computation | async-start | bytes 1310720 | tf_op jit(solution)/shard_map/all_to_all | solution.py:27
  328.0 360.4 %all-gather.10.cloned.1.call-start = ((), (), s32[]{:S(2)}) async-start(), calls=%async_computation.6 | async-start | bytes 5898240 | tf_op jit(solution)/shard_map/all_gather | solution.py:45
  328.8 15.4 %copy-start.4 = (s32[40,192]{1,0:T(8,128)S(1)}, s32[40,192]{1,0:T(8,128)}, u32[]{:S(2)}) copy-start(s32[40,192]{1,0:T(8,128)} %param.7) | copy-start | bytes 92164
  354.4 50.0 %copy-start.9 = (f32[2,40,2,192]{3,2,1,0:T(2,128)S(1)}, f32[2,40,2,192]{3,2,1,0:T(2,128)}, u32[]{:S(2)}) copy-start(f32[2,40,2,192]{3,2,1,0:T(2,128)} %param.9) | copy-start | bytes 368644
  404.4 0.7 copy-start.5
  629.8 13.4 %all-to-all-start.2 = ((f32[4,2,40,2,192]{4,1,2,3,0:T(2,128)}), f32[4,2,40,2,192]{4,1,2,3,0:T(2,128)S(1)}, u32[]{:S(2)}, u32[]{:S(2)}) async-start(f32[4,2,40,2,192]{4,1,2,3,0:T(2,128)} %broadcast_in_dim.10), calls=%async_computation.2 | async-start | bytes 1310720 | tf_op jit(solution)/shard_map/all_to_all | solution.py:27
  643.9 2.4 copy-start.2
  691.4 3.0 copy-start.1
  691.4 3.0 copy-start.3
  692.4 0.6 copy-start.6
  693.1 0.6 copy-start.7
  756.9 18.5 %all-to-all-start.3 = ((f32[64,2,2,192]{3,2,1,0:T(2,128)}), f32[64,2,2,192]{3,2,1,0:T(2,128)S(1)}, u32[]{:S(2)}, u32[]{:S(2)}) async-start(f32[64,2,2,192]{3,2,1,0:T(2,128)} %broadcast_in_dim.11), calls=%async_computation.3 | async-start | bytes 524288 | tf_op jit(solution)/shard_map/all_to_all | solution.py:27
Sparse Core Ops, SparseCore 0:
  10.4 308.0 all-gather.5
  320.8 304.2 all-gather.7
  626.9 61.3 all-gather.9
where the time goes:
time: 793 us; the launch traced here: 783 us
  waiting for transfers between devices  533 us (67%)
  blocking collectives  128 us (16%)
  matrix products  65.1 us (8%)
  local copies, waits for them, and re-layouts  17.5 us (2%)
  starting transfers between devices  17.1 us (2%)
  between operations  16.9 us (2%)
    all_gather x1, waiting for transfers between devices, per_device(): lax.all_gather(direction_low, RCV, axis=1, tiled=True)  308 us
    all_gather x1, waiting for transfers between devices, per_device(): lax.all_gather(focusing_low, RCV, axis=1, tiled=True)  163 us
    psum x10, blocking collectives, one_axis_at_a_time(): value = lax.psum(value, axis)  88.1 us
    all_gather x1, waiting for transfers between devices, all_blocks(): pieces = lax.all_gather(pieces, axes[k])  34.5 us
    dot_general x12, matrix products, contract_time(): return jnp.einsum('tf,frk->trk', table, values, precision=highest)  33.8 us
    all_to_all x3, waiting for transfers between devices, sent_to_all(): lax.all_to_all(jnp.broadcast_to(value[None], (count, *value.shape)), axis...  27.2 us
    dot_general x12, matrix products, contract_back(): return jnp.einsum('tf,trk->frk', table, values, precision=highest)  23.2 us
    all_gather x2, blocking collectives, all_blocks(): pieces = lax.all_gather(pieces, axes[k])  21.7 us
  transfers between devices with their start and end apart: 6, of which 6 were waited for; matrix products, arithmetic and copies ran while one was open for 8% of the time, Pallas kernels for 0%

commit v1 on v0

--- a/solution.py
+++ b/solution.py
@@ -14,6 +14,15 @@
 band_start = 5
 tiny = 1e-06
 highest = lax.Precision.HIGHEST
+bring_row_on = lambda x0: jnp.concatenate(
+    lax.all_to_all(
+        jnp.stack([x0 for _ in range(lax.axis_size(RCV))]),
+        axis_name=RCV,
+        split_axis=0,
+        concat_axis=0,
+    ),
+    axis=1,
+)
 
 
 def in_order(pieces, dim):
@@ -114,7 +123,7 @@
 
     direction_low = direction.astype(jnp.bfloat16)
     focusing_low = focusing.astype(jnp.bfloat16)
-    aimed_total = accumulate(lax.all_gather(direction_low, RCV, axis=1, tiled=True))
+    aimed_total = accumulate(bring_row_on(direction_low))
     direction_image = combine(aimed_total, False)
     image = gate(direction_image, False)
     gamma, curvature = (

time: 793 us -> 514 us (0.65)
  waiting for transfers between devices: 533 us -> 248 us
  starting transfers between devices: 17.1 us -> 30.8 us
    all_gather x1 -> x0, waiting for transfers between devices: 308 us -> none  [per_device(): lax.all_gather(direction_low, RCV, axis=1, tiled=True)]
    all_to_all x0 -> x1, waiting for transfers between devices: none -> 141 us  [lax.all_to_all(jnp.stack([x0 for _ in range(lax.axis_size(RCV))]), axis_n...]
    all_gather x1, waiting for transfers between devices: 163 us -> 47.2 us  [per_device(): lax.all_gather(focusing_low, RCV, axis=1, tiled=True)]
    all_to_all x0 -> x1, starting transfers between devices: none -> 13.1 us  [lax.all_to_all(jnp.stack([x0 for _ in range(lax.axis_size(RCV))]), axis_n...]
  transfers between devices with their start and end apart: 6 -> 6, of which waited for: 6 -> 6; matrix products, arithmetic and copies ran while one was open for 8% -> 12% of each run, Pallas kernels for 0% -> 0%
where the time goes in v1:
time: 514 us; the launch traced here: 510 us
  waiting for transfers between devices  248 us (48%)
  blocking collectives  124 us (24%)
  matrix products  62.6 us (12%)
  starting transfers between devices  30.8 us (6%)
  local copies, waits for them, and re-layouts  20.8 us (4%)
  between operations  17.3 us (3%)
  other arithmetic  6.25 us (1%)
    all_to_all x1, waiting for transfers between devices, lax.all_to_all(jnp.stack([x0 for _ in range(lax.axis_size(RCV))]), axis_n...  141 us
    psum x10, blocking collectives, one_axis_at_a_time(): value = lax.psum(value, axis)  83.6 us
    all_gather x1, waiting for transfers between devices, per_device(): lax.all_gather(focusing_low, RCV, axis=1, tiled=True)  47.2 us
    dot_general x12, matrix products, contract_time(): return jnp.einsum('tf,frk->trk', table, values, precision=highest)  33.8 us
    all_gather x1, waiting for transfers between devices, all_blocks(): pieces = lax.all_gather(pieces, axes[k])  32.7 us
    all_to_all x3, waiting for transfers between devices, sent_to_all(): lax.all_to_all(jnp.broadcast_to(value[None], (count, *value.shape)), axis...  27.4 us
    dot_general x12, matrix products, contract_back(): return jnp.einsum('tf,trk->frk', table, values, precision=highest)  23.2 us
    all_gather x2, blocking collectives, all_blocks(): pieces = lax.all_gather(pieces, axes[k])  20.7 us
  transfers between devices with their start and end apart: 6, of which 6 were waited for; matrix products, arithmetic and copies ran while one was open for 12% of the time, Pallas kernels for 0%

profile of v1, /device:TPU:4, one launch (start us, length us, event | category | flops | bytes accessed | tf_op | source)
XLA Modules:
  0.0 510.1 jit_solution(17805140955066823009)
XLA Ops:
  8.3 3.0 stack.32
  11.3 13.1 %all-to-all-start = ((bf16[64,2,40,2,192]{4,2,3,1,0:T(8,128)(2,1)}), bf16[64,2,40,2,192]{4,2,3,1,0:T(8,128)(2,1)}, u32[]{:S(2)}, u32[]{:S(2)}) async-start(bf16[64,2,40,2,192]{4,2,3,1,0:T(8,128)(2,1)} %stack.32), calls=%async_computation | async-start | bytes 10485760 | tf_op jit(solution)/shard_map/all_to_all | solution.py:18
  25.1 141.0 %all-to-all-done = bf16[64,2,40,2,192]{4,2,3,1,0:T(8,128)(2,1)} async-done(((bf16[64,2,40,2,192]{4,2,3,1,0:T(8,128)(2,1)}), bf16[64,2,40,2,192]{4,2,3,1,0:T(8,128)(2,1)}, u32[]{:S(2)}, u32[]{:S(2)}) %all-to-all-start) | async-done | bytes 3932192 | tf_op jit(solution)/shard_map/all_to_all | solution.py:18
  166.1 2.8 copy.167
  171.2 5.0 all-to-all-start.1
  177.2 12.5 %all-to-all-done.1 = f32[4,2,40,2,192]{4,1,2,3,0:T(2,128)S(1)} async-done(((f32[4,2,40,2,192]{4,1,2,3,0:T(2,128)}), f32[4,2,40,2,192]{4,1,2,3,0:T(2,128)S(1)}, u32[]{:S(2)}, u32[]{:S(2)}) %all-to-all-start.1) | async-done | bytes 491552 | tf_op jit(solution)/shard_map/all_to_all | solution.py:36
  190.4 2.4 fusion.6
  192.8 2.5 add_select_fusion.1
  195.3 1.4 fusion.114
  198.1 2.4 fusion.7
  200.5 2.5 subtract_select_fusion.1
  203.0 1.8 fusion.102
  206.9 7.1 %all-reduce.4 = (f32[]{:T(128)}, f32[]{:T(128)}) all-reduce(f32[]{:T(128)} %multiply_reduce_fusion.2, f32[]{:T(128)} %multiply_reduce_fusion.1), channel_id=1, replica_groups=mesh['freq_0'=2,'freq_1'=2,'rcv_0'=4,'rcv_1'=8,'rcv_2'=2] {'freq_0'}, use_global_device_ids=true, to_apply=%region_1.0 | all-reduce | flops 2 | bytes 16 | tf_op jit(solution)/shard_map/psum | solution.py:47
  213.9 3.1 all-reduce.3
  217.0 10.1 %all-reduce.1 = (f32[]{:T(128)}, f32[]{:T(128)}) all-reduce(f32[]{:T(128)} %get-tuple-element.38, f32[]{:T(128)} %get-tuple-element.39), channel_id=1, replica_groups=mesh['freq_0'=2,'freq_1'=2,'rcv_0'=4,'rcv_1'=8,'rcv_2'=2] {'rcv_0'}, use_global_device_ids=true, to_apply=%region_3.0 | all-reduce | flops 2 | bytes 16 | tf_op jit(solution)/shard_map/psum | solution.py:47
  227.1 14.8 %all-reduce = (f32[]{:T(128)}, f32[]{:T(128)}) all-reduce(f32[]{:T(128)} %get-tuple-element.34, f32[]{:T(128)} %get-tuple-element.35), channel_id=1, replica_groups=mesh['freq_0'=2,'freq_1'=2,'rcv_0'=4,'rcv_1'=8,'rcv_2'=2] {'rcv_1'}, use_global_device_ids=true, to_apply=%region_4.0 | all-reduce | flops 2 | bytes 16 | tf_op jit(solution)/shard_map/psum | solution.py:47
  241.9 5.5 %all-reduce.2 = (f32[]{:T(128)}, f32[]{:T(128)}) all-reduce(f32[]{:T(128)} %get-tuple-element.32, f32[]{:T(128)} %get-tuple-element.33), channel_id=1, replica_groups=mesh['freq_0'=2,'freq_1'=2,'rcv_0'=4,'rcv_1'=8,'rcv_2'=2] {'rcv_2'}, use_global_device_ids=true, to_apply=%region_5.0 | all-reduce | flops 2 | bytes 16 | tf_op jit(solution)/shard_map/psum | solution.py:47
  249.7 19.6 %all_to_all.25 = f32[4,2,40,2,192]{4,1,2,3,0:T(2,128)S(1)} all-to-all(f32[4,2,40,2,192]{4,1,2,3,0:T(2,128)S(1)} %broadcast_in_dim.9), channel_id=1, replica_groups=mesh['freq_0'=2,'freq_1'=2,'rcv_0'=4,'rcv_1'=8,'rcv_2'=2] {'freq_0','fre..., dimensions={0} | all-to-all | bytes 983040 | tf_op jit(solution)/shard_map/all_to_all | solution.py:36
  270.0 2.4 fusion.9
  272.4 2.5 subtract_select_fusion
  274.9 1.4 fusion.98
  276.3 2.4 fusion.8
  278.7 2.5 add_select_fusion
  282.6 1.6 fusion.100
  285.6 6.0 %all_gather.19 = bf16[2,2,40,2,192]{4,2,3,1,0:T(8,128)(2,1)S(1)} all-gather(bf16[1,2,40,2,192]{4,2,3,1,0:T(8,128)(2,1)S(1)} %copy.186), channel_id=1, replica_groups=mesh['freq_0'=2,'freq_1'=2,'rcv_0'=4,'rcv_1'=8,'rcv_2'=2] {'rcv_2'}, dimensions={0}, use_global_device_ids=true | all-gather | bytes 184320 | tf_op jit(solution)/shard_map/all_gather | solution.py:54
  291.6 14.8 %all-gather = bf16[8,2,40,2,192]{4,2,3,1,0:T(8,128)(2,1)} all-gather(bf16[2,2,40,2,192]{4,2,3,1,0:T(8,128)(2,1)S(1)} %all_gather.19), channel_id=2, replica_groups=mesh['freq_0'=2,'freq_1'=2,'rcv_0'=4,'rcv_1'=8,'rcv_2'=2] {'rcv_0'}, dimensions={0}, use_global_device_ids=true | all-gather | bytes 614400 | tf_op jit(solution)/shard_map/all_gather | solution.py:54
  306.4 47.2 %all-gather.5.cloned.1.call-done = bf16[2,2560,2,192]{3,1,2,0:T(8,128)(2,1)} async-done(((bf16[2,40,2,192]{3,1,2,0:T(8,128)(2,1)}), bf16[2,2560,2,192]{3,1,2,0:T(8,128)(2,1)}) %all-gather.5.cloned.1.call-update) | async-done | bytes 3932176 | tf_op jit(solution)/shard_map/all_gather | solution.py:141
  353.6 3.5 fusion
  358.3 5.0 all-to-all-start.3
  364.0 7.9 %all-to-all-done.3 = f32[4,2,40,2,192]{4,1,2,3,0:T(2,128)S(1)} async-done(((f32[4,2,40,2,192]{4,1,2,3,0:T(2,128)}), f32[4,2,40,2,192]{4,1,2,3,0:T(2,128)S(1)}, u32[]{:S(2)}, u32[]{:S(2)}) %all-to-all-start.3) | async-done | bytes 491552 | tf_op jit(solution)/shard_map/all_to_all | solution.py:36
  372.6 2.4 fusion.10
  375.0 3.9 fusion.11
  378.8 3.7 add_multiply_fusion
  382.6 32.7 %all-gather.7.cloned.1.call-done = bf16[32,2,2,40,2,192]{5,3,4,2,1,0:T(8,128)(2,1)} async-done(((bf16[4,2,2,40,2,192]{5,3,4,2,1,0:T(8,128)(2,1)}), bf16[32,2,2,40,2,192]{5,3,4,2,1,0:T(8,128)(2,1)}) %all-gather.7.cloned.1.call-update) | async-done | bytes 3932176 | tf_op jit(solution)/shard_map/all_gather | solution.py:54
  415.2 3.0 copy.187
  421.2 4.3 subtract_multiply_fusion
  425.5 7.1 %psum.115 = f32[]{:T(128)} all-reduce(f32[]{:T(128)} %multiply_reduce_fusion), channel_id=1, replica_groups=mesh['freq_0'=2,'freq_1'=2,'rcv_0'=4,'rcv_1'=8,'rcv_2'=2] {'freq_0'}, use_global_device_ids=true, to_apply=%region_13.0 | all-reduce | flops 1 | bytes 8 | tf_op jit(solution)/shard_map/psum | solution.py:47
  432.6 3.8 fusion.108
  436.3 3.3 psum.116
  439.6 3.7 fusion.94
  443.4 11.1 %psum.117 = f32[]{:T(128)} all-reduce(f32[]{:T(128)} %psum.116), channel_id=1, replica_groups=mesh['freq_0'=2,'freq_1'=2,'rcv_0'=4,'rcv_1'=8,'rcv_2'=2] {'rcv_0'}, use_global_device_ids=true, to_apply=%region_15.0 | all-reduce | flops 1 | bytes 8 | tf_op jit(solution)/shard_map/psum | solution.py:47
  454.4 2.0 fusion.96
  456.5 16.1 %psum.118 = f32[]{:T(128)} all-reduce(f32[]{:T(128)} %psum.117), channel_id=1, replica_groups=mesh['freq_0'=2,'freq_1'=2,'rcv_0'=4,'rcv_1'=8,'rcv_2'=2] {'rcv_1'}, use_global_device_ids=true, to_apply=%region_16.0 | all-reduce | flops 1 | bytes 8 | tf_op jit(solution)/shard_map/psum | solution.py:47
  472.6 2.0 fusion.106
  474.6 5.5 %psum.119 = f32[]{:T(128)} all-reduce(f32[]{:T(128)} %psum.118), channel_id=1, replica_groups=mesh['freq_0'=2,'freq_1'=2,'rcv_0'=4,'rcv_1'=8,'rcv_2'=2] {'rcv_2'}, use_global_device_ids=true, to_apply=%region_17.0 | all-reduce | flops 1 | bytes 8 | tf_op jit(solution)/shard_map/psum | solution.py:47
  483.8 7.5 %all-to-all-start.4 = ((f32[64,2,2,192]{3,2,1,0:T(2,128)}), f32[64,2,2,192]{3,2,1,0:T(2,128)S(1)}, u32[]{:S(2)}, u32[]{:S(2)}) async-start(f32[64,2,2,192]{3,2,1,0:T(2,128)} %broadcast_in_dim.11), calls=%async_computation.4 | async-start | bytes 524288 | tf_op jit(solution)/shard_map/all_to_all | solution.py:36
  491.3 1.7 copy.205
  495.4 6.9 %all-to-all-done.4 = f32[64,2,2,192]{3,2,1,0:T(2,128)S(1)} async-done(((f32[64,2,2,192]{3,2,1,0:T(2,128)}), f32[64,2,2,192]{3,2,1,0:T(2,128)S(1)}, u32[]{:S(2)}, u32[]{:S(2)}) %all-to-all-start.4) | async-done | bytes 196640 | tf_op jit(solution)/shard_map/all_to_all | solution.py:36
  (78 shorter events, 24.4 us)
Async XLA Ops:
  7.2 161.8 %copy-start = (bf16[2,2,40,2560]{3,2,1,0:T(8,128)(2,1)S(1)}, bf16[2,2,40,2560]{3,2,1,0:T(8,128)(2,1)}, u32[]{:S(2)}) copy-start(bf16[2,2,40,2560]{3,2,1,0:T(8,128)(2,1)} %param.6) | copy-start | bytes 2457604
  11.3 13.2 %copy-start.8 = (f32[2,40,2,192]{3,2,1,0:T(2,128)S(1)}, f32[2,40,2,192]{3,2,1,0:T(2,128)}, u32[]{:S(2)}) copy-start(f32[2,40,2,192]{3,2,1,0:T(2,128)} %param.8) | copy-start | bytes 368644
  11.3 154.9 %all-to-all-start = ((bf16[64,2,40,2,192]{4,2,3,1,0:T(8,128)(2,1)}), bf16[64,2,40,2,192]{4,2,3,1,0:T(8,128)(2,1)}, u32[]{:S(2)}, u32[]{:S(2)}) async-start(bf16[64,2,40,2,192]{4,2,3,1,0:T(8,128)(2,1)} %stack.32), calls=%async_computation | async-start | bytes 10485760 | tf_op jit(solution)/shard_map/all_to_all | solution.py:18
  24.4 329.2 %all-gather.5.cloned.1.call-start = ((), (), s32[]{:S(2)}) async-start(), calls=%async_computation.5 | async-start | bytes 5324800 | tf_op jit(solution)/shard_map/all_gather | solution.py:141
  170.0 6.4 %copy-start.9 = (f32[2,40,2,192]{3,2,1,0:T(2,128)S(1)}, f32[2,40,2,192]{3,2,1,0:T(2,128)}, u32[]{:S(2)}) copy-start(f32[2,40,2,192]{3,2,1,0:T(2,128)} %param.11) | copy-start | bytes 368644
  171.2 18.5 %all-to-all-start.1 = ((f32[4,2,40,2,192]{4,1,2,3,0:T(2,128)}), f32[4,2,40,2,192]{4,1,2,3,0:T(2,128)S(1)}, u32[]{:S(2)}, u32[]{:S(2)}) async-start(f32[4,2,40,2,192]{4,1,2,3,0:T(2,128)} %broadcast_in_dim.8), calls=%async_computation.1 | async-start | bytes 1310720 | tf_op jit(solution)/shard_map/all_to_all | solution.py:36
  176.2 239.0 %all-gather.7.cloned.1.call-start = ((), (), s32[]{:S(2)}) async-start(), calls=%async_computation.6 | async-start | bytes 5898240 | tf_op jit(solution)/shard_map/all_gather | solution.py:54
  177.2 15.6 %copy-start.4 = (s32[40,192]{1,0:T(8,128)S(1)}, s32[40,192]{1,0:T(8,128)}, u32[]{:S(2)}) copy-start(s32[40,192]{1,0:T(8,128)} %param.7) | copy-start | bytes 92164
  203.0 45.7 %copy-start.10 = (f32[2,40,2,192]{3,2,1,0:T(2,128)S(1)}, f32[2,40,2,192]{3,2,1,0:T(2,128)}, u32[]{:S(2)}) copy-start(f32[2,40,2,192]{3,2,1,0:T(2,128)} %param.9) | copy-start | bytes 368644
  248.8 0.7 copy-start.5
  358.3 13.6 %all-to-all-start.3 = ((f32[4,2,40,2,192]{4,1,2,3,0:T(2,128)}), f32[4,2,40,2,192]{4,1,2,3,0:T(2,128)S(1)}, u32[]{:S(2)}, u32[]{:S(2)}) async-start(f32[4,2,40,2,192]{4,1,2,3,0:T(2,128)} %broadcast_in_dim.10), calls=%async_computation.3 | async-start | bytes 1310720 | tf_op jit(solution)/shard_map/all_to_all | solution.py:36
  372.6 2.4 copy-start.2
  418.3 3.0 copy-start.1
  418.3 3.0 copy-start.3
  419.3 0.6 copy-start.6
  420.0 0.6 copy-start.7
  483.8 18.5 %all-to-all-start.4 = ((f32[64,2,2,192]{3,2,1,0:T(2,128)}), f32[64,2,2,192]{3,2,1,0:T(2,128)S(1)}, u32[]{:S(2)}, u32[]{:S(2)}) async-start(f32[64,2,2,192]{3,2,1,0:T(2,128)} %broadcast_in_dim.11), calls=%async_computation.4 | async-start | bytes 524288 | tf_op jit(solution)/shard_map/all_to_all | solution.py:36
Sparse Core Ops, SparseCore 0:
  27.5 326.0 all-gather.4
  355.4 59.7 all-gather.6
